TPU v7x, 256 devices: a whole 4x4x8 slice. The times are simulated.
256 devices in a mesh: row: 16 (over z, core), col: 16 (over y, x).
Axes of the slice: x: 4, y: 4, z: 8, core: 2. Of those that a mesh axis runs over, the one named last changes fastest.
Arguments:
- blocks: bfloat16 [16, 16, 5, 128, 8192], P('row', 'col'), may hold values from -6 to 6
- coords: int32 [16, 16, 5, 3], P('row', 'col'), may hold values from 0 to 15, as said below
- counts: int32 [16, 16], P('row', 'col'), may hold values from 1 to 5, as said below
- doc_factor: bfloat16 [32768, 128], P(('col', 'row')), may hold values from -6 to 6
- ctx_factor: bfloat16 [512, 128], P('col'), may hold values from -0.0625 to 0.0625
Outputs:
- mttkrp: float32 [32768, 128], P(('row', 'col'))
Inputs may be any that keep to these rules, and one draw needn't show every extreme that they name: coords[..., 0] lies in 0 to 15, coords[..., 1] in 0 to 15, coords[..., 2] in 0 to 7; slots at or past the device's count are ignored. `counts`: some device uses all 5 slots.
All inputs are finite; a program needn't handle non-finite values.
Results may differ from a plain program's by a relative error of at most 0.0029.
Values may be sent and summed in bfloat16 or wider, within the bound.
No kernel may reach another device: no remote copies, remote signals or barrier semaphores. Data moves between devices by JAX's collectives and lax.ppermute only.
A program may use at most 64 MiB of HBM per device.

v0:
```python
import jax
import jax.numpy as jnp
from jax import lax
from jax.sharding import PartitionSpec as P

BQ = 128
BD = 128
BK = 64
QBC = 1


def kr_table(brows, crows):
    table = brows[:, None, :].astype(jnp.float32) * crows[None, :, :].astype(jnp.float32)
    return table.reshape(brows.shape[0] * crows.shape[0], brows.shape[1]).astype(jnp.bfloat16)


def body(blocks, coords, counts, doc_factor, ctx_factor):
    doc_slab = lax.all_gather(doc_factor, "row", axis=0, tiled=True)
    ctx_all = lax.all_gather(ctx_factor, "col", axis=0, tiled=True)
    own_blocks = blocks[0, 0]
    own_coords = coords[0, 0]
    used = counts[0, 0]
    rank = doc_slab.shape[1]
    dev_rows = QBC * BQ
    all_rows = dev_rows * lax.axis_size("col")
    start = jnp.int32(0)
    empty = jnp.zeros((all_rows, rank), jnp.float32)

    def step(index, acc):
        place = own_coords[index]
        qstart = place[0] * BQ
        inside = jnp.logical_and(qstart >= start, qstart < start + all_rows)

        def add_term(inner):
            brows = lax.dynamic_slice_in_dim(doc_slab, place[1] * BD, BD, 0)
            crows = lax.dynamic_slice_in_dim(ctx_all, place[2] * BK, BK, 0)
            term = jnp.dot(
                own_blocks[index], kr_table(brows, crows), preferred_element_type=jnp.float32
            )
            local = jnp.clip(qstart, 0, all_rows - BQ)
            current = lax.dynamic_slice_in_dim(inner, local, BQ, 0)
            return lax.dynamic_update_slice_in_dim(inner, current + term, local, 0)

        return lax.cond(inside, add_term, lambda inner: inner, acc)

    partial_value = lax.fori_loop(0, used, step, empty)
    return lax.psum_scatter(partial_value, "col", scatter_dimension=0, tiled=True)


def solution(mesh):
    placed = (
        P("row", "col", None, None, None),
        P("row", "col", None, None),
        P("row", "col"),
        P(("col", "row"), None),
        P("col", None),
    )
    return jax.shard_map(
        body, mesh=mesh, in_specs=placed, out_specs=P(("row", "col"), None), check_vma=False
    )
```

profile of v0, /device:TPU:1, one launch (start us, length us, event | category | flops | bytes accessed | tf_op | source)
XLA Modules:
  0.0 171.8 jit_solution(1418539375337259537)
XLA Ops:
  6.5 0.0 reduce-scatter.2.cloned.1.call-start
  6.5 24.4 %all_gather.6 = bf16[2048,128]{1,0:T(8,128)(2,1)} all-gather(bf16[128,128]{1,0:T(8,128)(2,1)} %param.12), channel_id=1, replica_groups=mesh['row'=16,'col'=16] {'row'}, dimensions={0}, use_global_device_ids=true | all-gather | bytes 557056 | tf_op jit(solution)/shard_map/all_gather | solution.py:18
  30.9 18.8 %all_gather.7 = bf16[512,128]{1,0:T(8,128)(2,1)S(1)} all-gather(bf16[32,128]{1,0:T(8,128)(2,1)} %param.13), channel_id=1, replica_groups=mesh['row'=16,'col'=16] {'col'}, dimensions={0}, use_global_device_ids=true | all-gather | bytes 139264 | tf_op jit(solution)/shard_map/all_gather | solution.py:19
  49.7 0.8 copy.7
  50.5 0.1 broadcast_in_dim.2
  50.5 7.6 %while.13 = (s32[]{:T(128)}, f32[2048,128]{1,0:T(8,128)S(1)}, s32[]{:T(128)}, s32[5,3]{1,0:T(8,128)S(1)}, bf16[5,128,8192]{2,1,0:T(8,128)(2,1)}, /*index=5*/bf16...) while((s32[]{:T(128)}, f32[2048,128]{1,0:T(8,128)S(1)}, ...), condition=%wide.region_3.4_spmd, body=%wide.region_0.3_spmd.sunk | while | flops 270573568 | bytes 6799827 | solution.py:46
  51.3 6.2 %conditional.2 = (f32[2048,128]{1,0:T(8,128)S(1)}) conditional(s32[]{:T(128)} %convert_element_type.27, f32[2048,128]{1,0:T(8,128)S(1)} %get-tuple-element.150, (s32[]{:T(128)}, f32[2048,128]{1,0:T(8,128)S(1)}, s32[]{:T(128)}, bf16[5,128,8192]{2,1,0:T(8,128)(2,1)}, s32[1,3]{1,0:T(1,128)S(1)}, /*index=5*/bf16[2048,128]{1,0:T(8,128)(2,1)}, ...), branch_computations={%region_1.0_spmd, %region_2.2_spmd} | conditional | flops 270573568 | bytes 6799554 | solution.py:44
  51.3 0.6 fusion.7
  52.6 0.8 dynamic-slice_convert_fusion
  54.0 0.6 multiply_convert_fusion
  54.6 2.3 %fusion.3 = f32[128,128]{1,0:T(8,128)S(1)} fusion(bf16[8192,128]{1,0:T(8,128)(2,1)S(1)} %bitcast.18, bf16[5,128,8192]{2,1,0:T(8,128)(2,1)} %get-tuple-element.54, s32[]{:T(128)S(6)} %select_n.2, f32[2048,128]{1,0:T(8,128)S(1)} %get-tuple-element.52, s32[]{:T(128)S(6)} %min.3), kind=kOutput, calls=%fused_computation.4 | convolution fusion | flops 268451840 | bytes 4325384 | tf_op jit(solution)/shard_map/while/body/cond/branch_1_fun/dot_general | solution.py:37
  56.9 0.6 dynamic_update_slice.2
  58.2 0.0 copy-start
  58.2 1.0 copy-done
  59.1 0.0 reduce-scatter.2.cloned.1.call-update
  59.2 105.8 %reduce-scatter.2.cloned.1.call-done = f32[128,128]{1,0:T(8,128)} async-done(((f32[2048,128]{1,0:T(8,128)}), f32[128,128]{1,0:T(8,128)}) %reduce-scatter.2.cloned.1.call-update) | async-done | bytes 65552 | tf_op jit(solution)/shard_map/reduce_scatter | solution.py:47
  (2 shorter events, 0.0 us)
Async XLA Ops:
  6.5 158.4 %reduce-scatter.2.cloned.1.call-start = ((), (), s32[]{:S(2)}) async-start(), calls=%async_computation.1 | async-start | bytes 1114112 | tf_op jit(solution)/shard_map/reduce_scatter | solution.py:47
  58.2 1.0 copy-start
Sparse Core Ops, SparseCore 0:
  59.3 105.6 reduce-scatter.1
where the time goes:
time: 173 us; the launch traced here: 172 us
  waiting for transfers between devices  106 us (61%)
  blocking collectives  43.2 us (25%)
  between operations  13.4 us (8%)
  local copies, waits for them, and re-layouts  3.02 us (2%)
  loops' own time  2.7 us (2%)
  matrix products  2.29 us (1%)
    reduce_scatter x1, waiting for transfers between devices, body(): lax.psum_scatter(partial_value, 'col', scatter_dimension=0, tiled=True)  106 us
    all_gather x1, blocking collectives, body(): doc_slab = lax.all_gather(doc_factor, 'row', axis=0, tiled=True)  24.4 us
    all_gather x1, blocking collectives, body(): ctx_all = lax.all_gather(ctx_factor, 'col', axis=0, tiled=True)  18.8 us
  transfers between devices with their start and end apart: 1, of which 1 were waited for; matrix products, arithmetic and copies ran while one was open for 0% of the time, Pallas kernels for 0%

commit v1 on v0

--- a/solution.py
+++ b/solution.py
@@ -14,9 +14,15 @@
     return table.reshape(brows.shape[0] * crows.shape[0], brows.shape[1]).astype(jnp.bfloat16)
 
 
+def gather_rows(piece, axis):
+    copies = jnp.broadcast_to(piece[None], (lax.axis_size(axis),) + piece.shape)
+    gathered = lax.all_to_all(copies, axis, 0, 0, tiled=True)
+    return gathered.reshape(-1, piece.shape[-1])
+
+
 def body(blocks, coords, counts, doc_factor, ctx_factor):
-    doc_slab = lax.all_gather(doc_factor, "row", axis=0, tiled=True)
-    ctx_all = lax.all_gather(ctx_factor, "col", axis=0, tiled=True)
+    doc_slab = gather_rows(doc_factor, "row")
+    ctx_all = gather_rows(ctx_factor, "col")
     own_blocks = blocks[0, 0]
     own_coords = coords[0, 0]
     used = counts[0, 0]
@@ -44,7 +50,8 @@
         return lax.cond(inside, add_term, lambda inner: inner, acc)
 
     partial_value = lax.fori_loop(0, used, step, empty)
-    return lax.psum_scatter(partial_value, "col", scatter_dimension=0, tiled=True)
+    parts = partial_value.reshape(lax.axis_size("col"), dev_rows, rank)
+    return lax.all_to_all(parts, "col", 0, 0, tiled=True).sum(axis=0)
 
 
 def solution(mesh):

time: 173 us -> 101 us (0.58)
  waiting for transfers between devices: 106 us -> 16.5 us
  between operations: 13.4 us -> 0.02 us
  blocking collectives: 43.2 us -> 54.7 us
  starting transfers between devices: 0.01 us -> 10.6 us
  local copies, waits for them, and re-layouts: 3.02 us -> 5.45 us
  matrix products: 2.29 us -> 4.58 us
  other arithmetic: 1.4 us -> 3.49 us
  loops' own time: 2.7 us -> 4.75 us
    reduce_scatter x1 -> x0, waiting for transfers between devices: 106 us -> none  [body(): lax.psum_scatter(partial_value, 'col', scatter_dimension=0, tiled=True)]
    all_to_all x0 -> x2, blocking collectives: none -> 54.7 us  [the longest x1 40.5 us: body(): return lax.all_to_all(parts, 'col', 0, 0, tiled=True).sum(axis=0)]
    all_gather x2 -> x0, blocking collectives: 43.2 us -> none  [the longest x1 24.4 us: body(): doc_slab = lax.all_gather(doc_factor, 'row', axis=0, tiled=True)]
    all_to_all x0 -> x1, waiting for transfers between devices: none -> 16.5 us  [gather_rows(): gathered = lax.all_to_all(copies, axis, 0, 0, tiled=True)]
    all_to_all x0 -> x1, starting transfers between devices: none -> 10.6 us  [gather_rows(): gathered = lax.all_to_all(copies, axis, 0, 0, tiled=True)]
    broadcast_in_dim x0 -> x2, local copies, waits for them, and re-layouts: none -> 2.36 us  [gather_rows(): copies = jnp.broadcast_to(piece[None], (lax.axis_size(axis),) + piece.shape)]
    dot_general x1 -> x2, matrix products: 2.29 us -> 4.58 us  [add_term(): jnp.dot(own_blocks[index], kr_table(brows, crows), preferred_element_type...]
  transfers between devices with their start and end apart: 1 -> 1, of which waited for: 1 -> 1; matrix products, arithmetic and copies ran while one was open for 0% -> 1% of each run, Pallas kernels for 0% -> 0%
where the time goes in v1:
time: 101 us; the launch traced here: 100 us
  blocking collectives  54.7 us (54%)
  waiting for transfers between devices  16.5 us (16%)
  starting transfers between devices  10.6 us (10%)
  local copies, waits for them, and re-layouts  5.45 us (5%)
  loops' own time  4.75 us (5%)
  matrix products  4.58 us (5%)
  other arithmetic  3.49 us (3%)
    all_to_all x1, blocking collectives, body(): return lax.all_to_all(parts, 'col', 0, 0, tiled=True).sum(axis=0)  40.5 us
    all_to_all x1, waiting for transfers between devices, gather_rows(): gathered = lax.all_to_all(copies, axis, 0, 0, tiled=True)  16.5 us
    all_to_all x1, blocking collectives, gather_rows(): gathered = lax.all_to_all(copies, axis, 0, 0, tiled=True)  14.2 us
    all_to_all x1, starting transfers between devices, gather_rows(): gathered = lax.all_to_all(copies, axis, 0, 0, tiled=True)  10.6 us
    dot_general x2, matrix products, add_term(): jnp.dot(own_blocks[index], kr_table(brows, crows), preferred_element_type...  4.58 us
    another operation x2, loops' own time, step(): return lax.cond(inside, add_term, lambda inner: inner, acc)  2.64 us
    broadcast_in_dim x2, local copies, waits for them, and re-layouts, gather_rows(): copies = jnp.broadcast_to(piece[None], (lax.axis_size(axis),) + piece.shape)  2.36 us
    another operation x1, loops' own time, body(): partial_value = lax.fori_loop(0, used, step, empty)  2.11 us
  transfers between devices with their start and end apart: 1, of which 1 were waited for; matrix products, arithmetic and copies ran while one was open for 1% of the time, Pallas kernels for 0%

profile of v1, /device:TPU:1, one launch (start us, length us, event | category | flops | bytes accessed | tf_op | source)
XLA Modules:
  0.0 100.1 jit_solution(3695728379016058635)
XLA Ops:
  0.0 0.7 broadcast_in_dim.8
  0.7 14.2 %all_to_all.15 = bf16[16,32,128]{2,1,0:T(8,128)(2,1)S(1)} all-to-all(bf16[16,32,128]{2,1,0:T(8,128)(2,1)S(1)} %broadcast_in_dim.8), channel_id=1, replica_groups=mesh['row'=16,'col'=16] {'col'}, dimensions={0} | all-to-all | bytes 262144 | tf_op jit(solution)/shard_map/all_to_all | solution.py:19
  15.0 1.6 %broadcast_in_dim.7 = bf16[16,128,128]{2,1,0:T(8,128)(2,1)} broadcast(bf16[128,128]{1,0:T(8,128)(2,1)} %param.12), dimensions={1,2} | broadcast | bytes 557056 | tf_op jit(solution)/shard_map/broadcast_in_dim | solution.py:18
  16.6 10.6 %all-to-all-start = ((bf16[16,128,128]{2,1,0:T(8,128)(2,1)}), bf16[16,128,128]{2,1,0:T(8,128)(2,1)}, u32[]{:S(2)}, u32[]{:S(2)}) async-start(bf16[16,128,128]{2,1,0:T(8,128)(2,1)} %broadcast_in_dim.7), calls=%async_computation | async-start | bytes 1048576 | tf_op jit(solution)/shard_map/all_to_all | solution.py:19
  27.2 0.8 copy.7
  27.9 16.5 %all-to-all-done = bf16[16,128,128]{2,1,0:T(8,128)(2,1)} async-done(((bf16[16,128,128]{2,1,0:T(8,128)(2,1)}), bf16[16,128,128]{2,1,0:T(8,128)(2,1)}, u32[]{:S(2)}, u32[]{:S(2)}) %all-to-all-start) | async-done | bytes 524320 | tf_op jit(solution)/shard_map/all_to_all | solution.py:19
  44.5 0.1 broadcast_in_dim.6
  44.5 14.4 %while.13 = (s32[]{:T(128)}, f32[2048,128]{1,0:T(8,128)S(1)}, s32[]{:T(128)}, s32[5,3]{1,0:T(8,128)S(1)}, bf16[5,128,8192]{2,1,0:T(8,128)(2,1)}, /*index=5*/bf16...) while((s32[]{:T(128)}, f32[2048,128]{1,0:T(8,128)S(1)}, ...), condition=%wide.region_3.4_spmd, body=%wide.region_0.3_spmd.sunk | while | flops 270573568 | bytes 6799827 | solution.py:52
  45.3 6.0 %conditional.2 = (f32[2048,128]{1,0:T(8,128)S(1)}) conditional(s32[]{:T(128)} %convert_element_type.27, f32[2048,128]{1,0:T(8,128)S(1)} %get-tuple-element.150, (s32[]{:T(128)}, f32[2048,128]{1,0:T(8,128)S(1)}, s32[]{:T(128)}, bf16[5,128,8192]{2,1,0:T(8,128)(2,1)}, s32[1,3]{1,0:T(1,128)S(1)}, /*index=5*/bf16[2048,128]{1,0:T(8,128)(2,1)}, ...), branch_computations={%region_1.0_spmd, %region_2.2_spmd} | conditional | flops 270573568 | bytes 6799554 | solution.py:50
  45.3 0.7 fusion.7
  46.5 0.8 dynamic-slice_convert_fusion
  48.0 0.6 multiply_convert_fusion
  48.6 2.3 %fusion.3 = f32[128,128]{1,0:T(8,128)S(1)} fusion(bf16[8192,128]{1,0:T(8,128)(2,1)S(1)} %bitcast.21, bf16[5,128,8192]{2,1,0:T(8,128)(2,1)} %get-tuple-element.54, s32[]{:T(128)S(6)} %select_n.2, f32[2048,128]{1,0:T(8,128)S(1)} %get-tuple-element.52, s32[]{:T(128)S(6)} %min.3), kind=kOutput, calls=%fused_computation.4 | convolution fusion | flops 268451840 | bytes 4325384 | tf_op jit(solution)/shard_map/while/body/cond/branch_1_fun/dot_general | solution.py:43
  50.9 0.4 dynamic_update_slice.2
  52.0 6.2 %conditional.2 = (f32[2048,128]{1,0:T(8,128)S(1)}) conditional(s32[]{:T(128)} %convert_element_type.27, f32[2048,128]{1,0:T(8,128)S(1)} %get-tuple-element.150, (s32[]{:T(128)}, f32[2048,128]{1,0:T(8,128)S(1)}, s32[]{:T(128)}, bf16[5,128,8192]{2,1,0:T(8,128)(2,1)}, s32[1,3]{1,0:T(1,128)S(1)}, /*index=5*/bf16[2048,128]{1,0:T(8,128)(2,1)}, ...), branch_computations={%region_1.0_spmd, %region_2.2_spmd} | conditional | flops 270573568 | bytes 6799554 | solution.py:50
  52.1 0.7 fusion.7
  53.3 0.8 dynamic-slice_convert_fusion
  54.8 0.6 multiply_convert_fusion
  55.4 2.3 %fusion.3 = f32[128,128]{1,0:T(8,128)S(1)} fusion(bf16[8192,128]{1,0:T(8,128)(2,1)S(1)} %bitcast.21, bf16[5,128,8192]{2,1,0:T(8,128)(2,1)} %get-tuple-element.54, s32[]{:T(128)S(6)} %select_n.2, f32[2048,128]{1,0:T(8,128)S(1)} %get-tuple-element.52, s32[]{:T(128)S(6)} %min.3), kind=kOutput, calls=%fused_computation.4 | convolution fusion | flops 268451840 | bytes 4325384 | tf_op jit(solution)/shard_map/while/body/cond/branch_1_fun/dot_general | solution.py:43
  57.7 0.6 dynamic_update_slice.2
  58.9 40.5 %all_to_all.16 = f32[16,128,128]{2,1,0:T(8,128)S(1)} all-to-all(f32[16,128,128]{2,1,0:T(8,128)S(1)} %bitcast.23), channel_id=1, replica_groups=mesh['row'=16,'col'=16] {'col'}, dimensions={0} | all-to-all | bytes 2097152 | tf_op jit(solution)/shard_map/all_to_all | solution.py:54
  99.4 0.7 reduce_sum.9
  (4 shorter events, 0.0 us)
Async XLA Ops:
  16.6 27.9 %all-to-all-start = ((bf16[16,128,128]{2,1,0:T(8,128)(2,1)}), bf16[16,128,128]{2,1,0:T(8,128)(2,1)}, u32[]{:S(2)}, u32[]{:S(2)}) async-start(bf16[16,128,128]{2,1,0:T(8,128)(2,1)} %broadcast_in_dim.7), calls=%async_computation | async-start | bytes 1048576 | tf_op jit(solution)/shard_map/all_to_all | solution.py:19

commit v2 on v1

v2 whole, which is shorter than its diff:
```python
import jax
import jax.numpy as jnp
from jax import lax
from jax.experimental import pallas as pl
from jax.experimental.pallas import tpu as pltpu
from jax.sharding import PartitionSpec as P

BQ = 128
BD = 128
BK = 64
QBC = 1
DOC_CHUNK = 16


def gather_rows(piece, axis):
    copies = jnp.broadcast_to(piece[None], (lax.axis_size(axis),) + piece.shape)
    gathered = lax.all_to_all(copies, axis, 0, 0, tiled=True)
    return gathered.reshape(-1, piece.shape[-1])


def slot_kernel(coords_ref, count_ref, blocks_ref, doc_ref, ctx_ref, out_ref):
    slot = pl.program_id(0)
    n_doc = doc_ref.shape[0]
    n_ctx = ctx_ref.shape[0]
    n_q = out_ref.shape[0]

    @pl.when(slot == 0)
    def _():
        out_ref[...] = jnp.zeros_like(out_ref)

    @pl.when(slot < count_ref[0])
    def _():
        qid = jnp.clip(coords_ref[slot * 3], 0, n_q - 1)
        did = jnp.clip(coords_ref[slot * 3 + 1], 0, n_doc - 1)
        kid = jnp.clip(coords_ref[slot * 3 + 2], 0, n_ctx - 1)
        crows = ctx_ref[kid].astype(jnp.float32)
        width = DOC_CHUNK * BK
        acc = jnp.zeros(out_ref.shape[1:], jnp.float32)
        for chunk in range(BD // DOC_CHUNK):
            brows = doc_ref[did, pl.ds(chunk * DOC_CHUNK, DOC_CHUNK), :].astype(jnp.float32)
            table = (brows[:, None, :] * crows[None, :, :]).reshape(width, crows.shape[-1])
            acc += jnp.dot(
                blocks_ref[:, pl.ds(chunk * width, width)],
                table.astype(jnp.bfloat16),
                preferred_element_type=jnp.float32,
            )
        out_ref[qid] += acc


def slot_terms(own_blocks, own_coords, used, doc_blocks, ctx_blocks, n_q):
    slots, rows, width = own_blocks.shape
    rank = doc_blocks.shape[-1]

    def block_map(s, coords_ref, count_ref):
        return (jnp.minimum(s, jnp.maximum(count_ref[0] - 1, 0)), 0, 0)

    grid_spec = pltpu.PrefetchScalarGridSpec(
        num_scalar_prefetch=2,
        grid=(slots,),
        in_specs=[
            pl.BlockSpec((None, rows, width), block_map),
            pl.BlockSpec(doc_blocks.shape, lambda s, c, n: (0, 0, 0)),
            pl.BlockSpec(ctx_blocks.shape, lambda s, c, n: (0, 0, 0)),
        ],
        out_specs=pl.BlockSpec((n_q, rows, rank), lambda s, c, n: (0, 0, 0)),
    )
    cost = pl.CostEstimate(
        flops=2 * slots * rows * width * rank,
        bytes_accessed=own_blocks.size * 2 + n_q * rows * rank * 4,
        transcendentals=0,
    )
    return pl.pallas_call(
        slot_kernel,
        grid_spec=grid_spec,
        out_shape=jax.ShapeDtypeStruct((n_q, rows, rank), jnp.float32),
        compiler_params=pltpu.CompilerParams(dimension_semantics=("arbitrary",)),
        cost_estimate=cost,
    )(own_coords.reshape(-1), used.reshape(-1), own_blocks, doc_blocks, ctx_blocks)


def body(blocks, coords, counts, doc_factor, ctx_factor):
    doc_slab = gather_rows(doc_factor, "row")
    ctx_all = gather_rows(ctx_factor, "col")
    rank = doc_slab.shape[1]
    n_q = QBC * lax.axis_size("col")
    doc_blocks = doc_slab.reshape(-1, BD, rank)
    ctx_blocks = ctx_all.reshape(-1, BK, rank)
    parts = slot_terms(blocks[0, 0], coords[0, 0], counts[0], doc_blocks, ctx_blocks, n_q)
    return lax.all_to_all(parts, "col", 0, 0, tiled=True).sum(axis=0)


def solution(mesh):
    placed = (
        P("row", "col", None, None, None),
        P("row", "col", None, None),
        P("row", "col"),
        P(("col", "row"), None),
        P("col", None),
    )
    return jax.shard_map(
        body, mesh=mesh, in_specs=placed, out_specs=P(("row", "col"), None), check_vma=False
    )
```

time: 101 us -> 74 us (0.73)
  blocking collectives: 54.7 us -> 37.2 us
  loops' own time: 4.75 us -> 0 us
  matrix products: 4.58 us -> 0 us
  Pallas kernels: 0 us -> 4.31 us
  other arithmetic: 3.49 us -> 0.69 us
  waiting for transfers between devices: 16.5 us -> 15.2 us
    all_to_all x1, blocking collectives: 40.5 us -> 22.9 us  [body(): return lax.all_to_all(parts, 'col', 0, 0, tiled=True).sum(axis=0)]
    another operation x3 -> x0, loops' own time: 4.75 us -> none  [the longest x2 2.64 us: step(): return lax.cond(inside, add_term, lambda inner: inner, acc)]
    dot_general x2 -> x0, matrix products: 4.58 us -> none  [add_term(): jnp.dot(own_blocks[index], kr_table(brows, crows), preferred_element_type...]
    pallas_call x0 -> x1, Pallas kernels: none -> 4.31 us  [slot_terms(): pl.pallas_call(slot_kernel, grid_spec=grid_spec, out_shape=jax.ShapeDtype...]
    convert_element_type x6 -> x0, other arithmetic: 2.8 us -> none  [the longest x2 1.54 us: kr_table(): brows[:, None, :].astype(jnp.float32)]
    unnamed x0 -> x3, local copies, waits for them, and re-layouts: none -> 1.58 us
    all_to_all x1, waiting for transfers between devices: 16.5 us -> 15.2 us  [gather_rows(): gathered = lax.all_to_all(copies, axis, 0, 0, tiled=True)]
    slice x2 -> x0, local copies, waits for them, and re-layouts: 1.3 us -> none  [add_term(): brows = lax.dynamic_slice_in_dim(doc_slab, place[1] * BD, BD, 0)]
  transfers between devices with their start and end apart: 1 -> 1, of which waited for: 1 -> 1; matrix products, arithmetic and copies ran while one was open for 1% -> 2% of each run, Pallas kernels for 0% -> 0%
where the time goes in v2:
time: 74 us; the launch traced here: 73.2 us
  blocking collectives  37.2 us (50%)
  waiting for transfers between devices  15.2 us (21%)
  starting transfers between devices  10.6 us (14%)
  local copies, waits for them, and re-layouts  4.53 us (6%)
  Pallas kernels  4.31 us (6%)
    all_to_all x1, blocking collectives, body(): return lax.all_to_all(parts, 'col', 0, 0, tiled=True).sum(axis=0)  22.9 us
    all_to_all x1, waiting for transfers between devices, gather_rows(): gathered = lax.all_to_all(copies, axis, 0, 0, tiled=True)  15.2 us
    all_to_all x1, blocking collectives, gather_rows(): gathered = lax.all_to_all(copies, axis, 0, 0, tiled=True)  14.3 us
    all_to_all x1, starting transfers between devices, gather_rows(): gathered = lax.all_to_all(copies, axis, 0, 0, tiled=True)  10.6 us
    pallas_call x1, Pallas kernels, slot_terms(): pl.pallas_call(slot_kernel, grid_spec=grid_spec, out_shape=jax.ShapeDtype...  4.31 us
    broadcast_in_dim x2, local copies, waits for them, and re-layouts, gather_rows(): copies = jnp.broadcast_to(piece[None], (lax.axis_size(axis),) + piece.shape)  2.36 us
    unnamed x3, local copies, waits for them, and re-layouts  1.58 us
  transfers between devices with their start and end apart: 1, of which 1 were waited for; matrix products, arithmetic and copies ran while one was open for 2% of the time, Pallas kernels for 0%

profile of v2, /device:TPU:1, one launch (start us, length us, event | category | flops | bytes accessed | tf_op | source)
XLA Modules:
  0.0 73.2 jit_solution(16475167081331718348)
XLA Ops:
  0.0 0.7 broadcast_in_dim.5
  0.7 14.3 %all_to_all.15 = bf16[16,32,128]{2,1,0:T(8,128)(2,1)} all-to-all(bf16[16,32,128]{2,1,0:T(8,128)(2,1)S(1)} %broadcast_in_dim.5), channel_id=1, replica_groups=mesh['row'=16,'col'=16] {'col'}, dimensions={0} | all-to-all | bytes 262144 | tf_op jit(solution)/shard_map/all_to_all | solution.py:17
  15.1 1.6 %broadcast_in_dim.4 = bf16[16,128,128]{2,1,0:T(8,128)(2,1)} broadcast(bf16[128,128]{1,0:T(8,128)(2,1)} %param.8), dimensions={1,2} | broadcast | bytes 557056 | tf_op jit(solution)/shard_map/broadcast_in_dim | solution.py:16
  16.7 10.6 %all-to-all-start = ((bf16[16,128,128]{2,1,0:T(8,128)(2,1)}), bf16[16,128,128]{2,1,0:T(8,128)(2,1)S(1)}, u32[]{:S(2)}, u32[]{:S(2)}) async-start(bf16[16,128,128]{2,1,0:T(8,128)(2,1)} %broadcast_in_dim.4), calls=%async_computation | async-start | bytes 1048576 | tf_op jit(solution)/shard_map/all_to_all | solution.py:17
  27.9 0.8 %copy.7 = s32[1,1,5,3]{3,2,1,0:T(8,128)S(1)} copy(s32[1,1,5,3]{2,1,3,0:T(1,128)} %param.6) | data formatting | bytes 120 | tf_op args[1]
  28.7 0.6 reshape_squeeze.3.coords_ref
  29.3 15.2 %all-to-all-done.doc_ref = bf16[16,128,128]{2,1,0:T(8,128)(2,1)S(1)} async-done(((bf16[16,128,128]{2,1,0:T(8,128)(2,1)}), bf16[16,128,128]{2,1,0:T(8,128)(2,1)S(1)}, u32[]{:S(2)}, u32[]{:S(2)}) %all-to-all-start) | async-done | bytes 524320 | tf_op jit(solution)/shard_map/all_to_all | solution.py:17
  44.5 0.0 copy-start
  44.5 0.8 %copy-done = bf16[16,128,128]{2,1,0:T(8,128)(2,1)} copy-done((bf16[16,128,128]{2,1,0:T(8,128)(2,1)}, bf16[16,128,128]{2,1,0:T(8,128)(2,1)S(1)}, u32[]{:S(2)}) %copy-start) | copy-done | bytes 524312
  45.3 4.3 %shard_map.55 = f32[16,128,128]{2,1,0:T(8,128)} custom-call(s32[15]{0:T(128)} %reshape_squeeze.3.coords_ref, s32[1]{0:T(128)} %bitcast.3.count_ref, bf16[5,128,8192]{2,1,0:T(8,128)(2,1)} %bitcast.4, bf16[16,128,128]{2,1,0:T(8,128)(2,1)} %copy-done, bf16[8,64,128]{2,1,0:T(8,128)(2,1)} %bitcast.5), custom_call_target="tpu_custom_call" | custom-call | flops 1342177280 | bytes 11534336 | tf_op jit(solution)/shard_map/pallas_call | solution.py:72
  49.6 22.9 %all_to_all.16 = f32[16,128,128]{2,1,0:T(8,128)S(1)} all-to-all(f32[16,128,128]{2,1,0:T(8,128)} %shard_map.55), channel_id=1, replica_groups=mesh['row'=16,'col'=16] {'col'}, dimensions={0} | all-to-all | bytes 2097152 | tf_op jit(solution)/shard_map/all_to_all | solution.py:89
  72.5 0.7 reduce_sum.9
Async XLA Ops:
  16.7 27.8 %all-to-all-start = ((bf16[16,128,128]{2,1,0:T(8,128)(2,1)}), bf16[16,128,128]{2,1,0:T(8,128)(2,1)S(1)}, u32[]{:S(2)}, u32[]{:S(2)}) async-start(bf16[16,128,128]{2,1,0:T(8,128)(2,1)} %broadcast_in_dim.4), calls=%async_computation | async-start | bytes 1048576 | tf_op jit(solution)/shard_map/all_to_all | solution.py:17
  44.5 0.8 %copy-start = (bf16[16,128,128]{2,1,0:T(8,128)(2,1)}, bf16[16,128,128]{2,1,0:T(8,128)(2,1)S(1)}, u32[]{:S(2)}) copy-start(bf16[16,128,128]{2,1,0:T(8,128)(2,1)S(1)} %all-to-all-done.doc_ref) | copy-start | bytes 1572868

commit v3 on v2

--- a/solution.py
+++ b/solution.py
@@ -33,15 +33,15 @@
         qid = jnp.clip(coords_ref[slot * 3], 0, n_q - 1)
         did = jnp.clip(coords_ref[slot * 3 + 1], 0, n_doc - 1)
         kid = jnp.clip(coords_ref[slot * 3 + 2], 0, n_ctx - 1)
-        crows = ctx_ref[kid].astype(jnp.float32)
+        crows = ctx_ref[kid]
         width = DOC_CHUNK * BK
         acc = jnp.zeros(out_ref.shape[1:], jnp.float32)
         for chunk in range(BD // DOC_CHUNK):
-            brows = doc_ref[did, pl.ds(chunk * DOC_CHUNK, DOC_CHUNK), :].astype(jnp.float32)
+            brows = doc_ref[did, pl.ds(chunk * DOC_CHUNK, DOC_CHUNK), :]
             table = (brows[:, None, :] * crows[None, :, :]).reshape(width, crows.shape[-1])
             acc += jnp.dot(
                 blocks_ref[:, pl.ds(chunk * width, width)],
-                table.astype(jnp.bfloat16),
+                table,
                 preferred_element_type=jnp.float32,
             )
         out_ref[qid] += acc
@@ -79,7 +79,7 @@
 
 
 def body(blocks, coords, counts, doc_factor, ctx_factor):
-    doc_slab = gather_rows(doc_factor, "row")
+    doc_slab = lax.all_gather(doc_factor, "row", axis=0, tiled=True)
     ctx_all = gather_rows(ctx_factor, "col")
     rank = doc_slab.shape[1]
     n_q = QBC * lax.axis_size("col")

time: 74 us -> 66.5 us (0.90)
  waiting for transfers between devices: 15.2 us -> 0.01 us
  blocking collectives: 37.2 us -> 48.2 us
  starting transfers between devices: 10.6 us -> 7.57 us
  local copies, waits for them, and re-layouts: 4.53 us -> 3.37 us
    all_gather x0 -> x1, blocking collectives: none -> 23.8 us  [body(): doc_slab = lax.all_gather(doc_factor, 'row', axis=0, tiled=True)]
    all_to_all x1, waiting for transfers between devices: 15.2 us -> 0.01 us  [gather_rows(): gathered = lax.all_to_all(copies, axis, 0, 0, tiled=True)]
    all_to_all x1 -> x0, blocking collectives: 14.3 us -> none  [gather_rows(): gathered = lax.all_to_all(copies, axis, 0, 0, tiled=True)]
    all_to_all x1, starting transfers between devices: 10.6 us -> 7.57 us  [gather_rows(): gathered = lax.all_to_all(copies, axis, 0, 0, tiled=True)]
    all_to_all x1, blocking collectives: 22.9 us -> 24.3 us  [body(): return lax.all_to_all(parts, 'col', 0, 0, tiled=True).sum(axis=0)]
    broadcast_in_dim x2 -> x1, local copies, waits for them, and re-layouts: 2.36 us -> 1.36 us  [gather_rows(): copies = jnp.broadcast_to(piece[None], (lax.axis_size(axis),) + piece.shape)]
  transfers between devices with their start and end apart: 1 -> 1, of which waited for: 1 -> 0; matrix products, arithmetic and copies ran while one was open for 2% -> 2% of each run, Pallas kernels for 0% -> 0%
where the time goes in v3:
time: 66.5 us; the launch traced here: 65.5 us
  blocking collectives  48.2 us (72%)
  starting transfers between devices  7.57 us (11%)
  Pallas kernels  5 us (8%)
  local copies, waits for them, and re-layouts  3.37 us (5%)
  other arithmetic  0.69 us (1%)
  between operations  0.67 us (1%)
    all_to_all x1, blocking collectives, body(): return lax.all_to_all(parts, 'col', 0, 0, tiled=True).sum(axis=0)  24.3 us
    all_gather x1, blocking collectives, body(): doc_slab = lax.all_gather(doc_factor, 'row', axis=0, tiled=True)  23.8 us
    all_to_all x1, starting transfers between devices, gather_rows(): gathered = lax.all_to_all(copies, axis, 0, 0, tiled=True)  7.57 us
    pallas_call x1, Pallas kernels, slot_terms(): pl.pallas_call(slot_kernel, grid_spec=grid_spec, out_shape=jax.ShapeDtype...  5 us
    unnamed x3, local copies, waits for them, and re-layouts  1.42 us
    broadcast_in_dim x1, local copies, waits for them, and re-layouts, gather_rows(): copies = jnp.broadcast_to(piece[None], (lax.axis_size(axis),) + piece.shape)  1.36 us
  transfers between devices with their start and end apart: 1, of which 0 were waited for; matrix products, arithmetic and copies ran while one was open for 2% of the time, Pallas kernels for 0%

profile of v3, /device:TPU:1, one launch (start us, length us, event | category | flops | bytes accessed | tf_op | source)
XLA Modules:
  0.0 65.5 jit_solution(702551717912181209)
XLA Ops:
  0.0 1.4 %broadcast_in_dim.2 = bf16[16,32,128]{2,1,0:T(8,128)(2,1)} broadcast(bf16[32,128]{1,0:T(8,128)(2,1)} %param.9), dimensions={1,2} | broadcast | bytes 139264 | tf_op jit(solution)/shard_map/broadcast_in_dim | solution.py:16
  1.4 7.6 %all-to-all-start = ((bf16[16,32,128]{2,1,0:T(8,128)(2,1)}), bf16[16,32,128]{2,1,0:T(8,128)(2,1)S(1)}, u32[]{:S(2)}, u32[]{:S(2)}) async-start(bf16[16,32,128]{2,1,0:T(8,128)(2,1)} %broadcast_in_dim.2), calls=%async_computation | async-start | bytes 262144 | tf_op jit(solution)/shard_map/all_to_all | solution.py:17
  8.9 23.8 %all_gather.3 = bf16[2048,128]{1,0:T(8,128)(2,1)} all-gather(bf16[128,128]{1,0:T(8,128)(2,1)} %param.8), channel_id=1, replica_groups=mesh['row'=16,'col'=16] {'row'}, dimensions={0}, use_global_device_ids=true | all-gather | bytes 557056 | tf_op jit(solution)/shard_map/all_gather | solution.py:82
  33.4 0.8 %copy.7 = s32[1,1,5,3]{3,2,1,0:T(8,128)S(1)} copy(s32[1,1,5,3]{2,1,3,0:T(1,128)} %param.6) | data formatting | bytes 120 | tf_op args[1]
  34.2 0.6 reshape_squeeze.3.coords_ref
  34.8 0.0 all-to-all-done
  34.8 0.0 copy-start
  34.8 0.6 copy-done
  35.5 5.0 %shard_map.55 = f32[16,128,128]{2,1,0:T(8,128)} custom-call(s32[15]{0:T(128)} %reshape_squeeze.3.coords_ref, s32[1]{0:T(128)} %bitcast.4.count_ref, bf16[5,128,8192]{2,1,0:T(8,128)(2,1)} %bitcast.5, bf16[16,128,128]{2,1,0:T(8,128)(2,1)} %bitcast.6, bf16[8,64,128]{2,1,0:T(8,128)(2,1)} %bitcast.7), custom_call_target="tpu_custom_call" | custom-call | flops 1342177280 | bytes 11534336 | tf_op jit(solution)/shard_map/pallas_call | solution.py:72
  40.5 24.3 %all_to_all.10 = f32[16,128,128]{2,1,0:T(8,128)S(1)} all-to-all(f32[16,128,128]{2,1,0:T(8,128)} %shard_map.55), channel_id=1, replica_groups=mesh['row'=16,'col'=16] {'col'}, dimensions={0} | all-to-all | bytes 2097152 | tf_op jit(solution)/shard_map/all_to_all | solution.py:89
  64.8 0.7 %reduce_sum.9 = f32[128,128]{1,0:T(8,128)} reduce(f32[16,128,128]{2,1,0:T(8,128)S(1)} %all_to_all.10, f32[]{:T(128)} %constant.0.clone.1), dimensions={0}, to_apply=%region_0.0 | reduce | flops 245760 | bytes 1114116 | tf_op jit(solution)/shard_map/reduce_sum | solution.py:89
Async XLA Ops:
  1.4 33.4 %all-to-all-start = ((bf16[16,32,128]{2,1,0:T(8,128)(2,1)}), bf16[16,32,128]{2,1,0:T(8,128)(2,1)S(1)}, u32[]{:S(2)}, u32[]{:S(2)}) async-start(bf16[16,32,128]{2,1,0:T(8,128)(2,1)} %broadcast_in_dim.2), calls=%async_computation | async-start | bytes 262144 | tf_op jit(solution)/shard_map/all_to_all | solution.py:17
  34.8 0.6 copy-start

commit v4 on v3

v4 whole, which is shorter than its diff:
```python
import jax
import jax.numpy as jnp
from jax import lax
from jax.experimental import pallas as pl
from jax.experimental.pallas import tpu as pltpu
from jax.sharding import PartitionSpec as P

BQ = 128
BD = 128
BK = 64
QBC = 1
DOC_CHUNK = 16


def gather_rows(piece, axis):
    copies = jnp.broadcast_to(piece[None], (lax.axis_size(axis),) + piece.shape)
    gathered = lax.all_to_all(copies, axis, 0, 0, tiled=True)
    return gathered.reshape(-1, piece.shape[-1])


def slot_kernel(coords_ref, count_ref, blocks_hbm, doc_ref, ctx_ref, out_ref, held, sems):
    n_doc = doc_ref.shape[0]
    n_ctx = ctx_ref.shape[0]
    n_q = out_ref.shape[0]
    slots = blocks_hbm.shape[0]
    pieces = held.shape[1]
    piece = held.shape[-1]
    used = jnp.clip(count_ref[0], 0, slots)

    def fetch(slot, part):
        return pltpu.make_async_copy(
            blocks_hbm.at[slot, :, pl.ds(part * piece, piece)],
            held.at[slot % 2, part],
            sems.at[slot % 2, part],
        )

    @pl.when(used > 0)
    def _():
        for part in range(pieces):
            fetch(0, part).start()

    out_ref[...] = jnp.zeros_like(out_ref)

    def step(slot, carry):
        @pl.when(slot + 1 < used)
        def _():
            for part in range(pieces):
                fetch(slot + 1, part).start()

        qid = jnp.clip(coords_ref[0, slot], 0, n_q - 1)
        did = jnp.clip(coords_ref[1, slot], 0, n_doc - 1)
        kid = jnp.clip(coords_ref[2, slot], 0, n_ctx - 1)
        crows = ctx_ref[kid]
        width = DOC_CHUNK * BK
        acc = jnp.zeros(out_ref.shape[1:], jnp.float32)
        for part in range(pieces):
            fetch(slot, part).wait()
            for sub in range(piece // width):
                first = (part * piece + sub * width) // BK
                brows = doc_ref[did, pl.ds(first, DOC_CHUNK), :]
                table = (brows[:, None, :] * crows[None, :, :]).reshape(width, crows.shape[-1])
                acc += jnp.dot(
                    held[slot % 2, part, :, pl.ds(sub * width, width)],
                    table,
                    preferred_element_type=jnp.float32,
                )
        out_ref[qid] += acc
        return carry

    lax.fori_loop(0, used, step, 0)


def slot_terms(own_blocks, own_coords, used, doc_blocks, ctx_blocks, n_q):
    slots, rows, width = own_blocks.shape
    rank = doc_blocks.shape[-1]
    pieces = 4
    cost = pl.CostEstimate(
        flops=2 * slots * rows * width * rank,
        bytes_accessed=own_blocks.size * 2 + n_q * rows * rank * 4,
        transcendentals=0,
    )
    return pl.pallas_call(
        slot_kernel,
        in_specs=[
            pl.BlockSpec(memory_space=pltpu.SMEM),
            pl.BlockSpec(memory_space=pltpu.SMEM),
            pl.BlockSpec(memory_space=pl.ANY),
            pl.BlockSpec(memory_space=pltpu.VMEM),
            pl.BlockSpec(memory_space=pltpu.VMEM),
        ],
        out_specs=pl.BlockSpec(memory_space=pltpu.VMEM),
        out_shape=jax.ShapeDtypeStruct((n_q, rows, rank), jnp.float32),
        scratch_shapes=[
            pltpu.VMEM((2, pieces, rows, width // pieces), own_blocks.dtype),
            pltpu.SemaphoreType.DMA((2, pieces)),
        ],
        cost_estimate=cost,
    )(own_coords.T, used.reshape(-1), own_blocks, doc_blocks, ctx_blocks)


def body(blocks, coords, counts, doc_factor, ctx_factor):
    doc_slab = lax.all_gather(doc_factor, "row", axis=0, tiled=True)
    ctx_all = gather_rows(ctx_factor, "col")
    rank = doc_slab.shape[1]
    n_q = QBC * lax.axis_size("col")
    doc_blocks = doc_slab.reshape(-1, BD, rank)
    ctx_blocks = ctx_all.reshape(-1, BK, rank)
    parts = slot_terms(blocks[0, 0], coords[0, 0], counts[0], doc_blocks, ctx_blocks, n_q)
    return lax.all_to_all(parts, "col", 0, 0, tiled=True).sum(axis=0)


def solution(mesh):
    placed = (
        P("row", "col", None, None, None),
        P("row", "col", None, None),
        P("row", "col"),
        P(("col", "row"), None),
        P("col", None),
    )
    return jax.shard_map(
        body, mesh=mesh, in_specs=placed, out_specs=P(("row", "col"), None), check_vma=False
    )
```

time: 66.5 us -> 69.1 us (1.039)
  blocking collectives: 48.2 us -> 50.9 us
    all_to_all x1, blocking collectives: 24.3 us -> 27 us  [body(): return lax.all_to_all(parts, 'col', 0, 0, tiled=True).sum(axis=0)]
where the time goes in v4:
time: 69.1 us; the launch traced here: 68.7 us
  blocking collectives  50.9 us (74%)
  starting transfers between devices  7.57 us (11%)
  Pallas kernels  5.58 us (8%)
  local copies, waits for them, and re-layouts  3.27 us (5%)
    all_to_all x1, blocking collectives, body(): return lax.all_to_all(parts, 'col', 0, 0, tiled=True).sum(axis=0)  27 us
    all_gather x1, blocking collectives, body(): doc_slab = lax.all_gather(doc_factor, 'row', axis=0, tiled=True)  23.8 us
    all_to_all x1, starting transfers between devices, gather_rows(): gathered = lax.all_to_all(copies, axis, 0, 0, tiled=True)  7.57 us
    pallas_call x1, Pallas kernels, slot_terms(): pl.pallas_call(slot_kernel, in_specs=[pl.BlockSpec(memory_space=pltpu.SME...  5.58 us
    unnamed x3, local copies, waits for them, and re-layouts  1.91 us
  transfers between devices with their start and end apart: 1, of which 0 were waited for; matrix products, arithmetic and copies ran while one was open for 2% of the time, Pallas kernels for 0%

profile of v4, /device:TPU:1, one launch (start us, length us, event | category | flops | bytes accessed | tf_op | source)
XLA Modules:
  0.0 68.7 jit_solution(12580750889662567182)
XLA Ops:
  0.0 1.4 %broadcast_in_dim.2 = bf16[16,32,128]{2,1,0:T(8,128)(2,1)} broadcast(bf16[32,128]{1,0:T(8,128)(2,1)} %param.9), dimensions={1,2} | broadcast | bytes 139264 | tf_op jit(solution)/shard_map/broadcast_in_dim | solution.py:16
  1.4 7.6 %all-to-all-start = ((bf16[16,32,128]{2,1,0:T(8,128)(2,1)}), bf16[16,32,128]{2,1,0:T(8,128)(2,1)S(1)}, u32[]{:S(2)}, u32[]{:S(2)}) async-start(bf16[16,32,128]{2,1,0:T(8,128)(2,1)} %broadcast_in_dim.2), calls=%async_computation | async-start | bytes 262144 | tf_op jit(solution)/shard_map/all_to_all | solution.py:17
  8.9 23.8 %all_gather.3 = bf16[2048,128]{1,0:T(8,128)(2,1)} all-gather(bf16[128,128]{1,0:T(8,128)(2,1)} %param.8), channel_id=1, replica_groups=mesh['row'=16,'col'=16] {'row'}, dimensions={0}, use_global_device_ids=true | all-gather | bytes 557056 | tf_op jit(solution)/shard_map/all_gather | solution.py:102
  33.4 1.3 %copy.8 = s32[1,1,5,3]{2,3,1,0:T(4,128)} copy(s32[1,1,5,3]{2,1,3,0:T(1,128)} %param.6) | data formatting | bytes 120
  34.7 0.0 all-to-all-done
  34.7 0.0 copy-start
  34.7 0.6 copy-done
  35.4 5.6 %shard_map.55 = f32[16,128,128]{2,1,0:T(8,128)} custom-call(s32[3,5]{1,0:T(4,128)} %bitcast.13, s32[1]{0:T(128)} %bitcast.9.count_ref, bf16[5,128,8192]{2,1,0:T(8,128)(2,1)} %bitcast.10, bf16[16,128,128]{2,1,0:T(8,128)(2,1)} %bitcast.11, bf16[8,64,128]{2,1,0:T(8,128)(2,1)} %bitcast.12), custom_call_target="tpu_custom_call" | custom-call | flops 1342177280 | bytes 11534336 | tf_op jit(solution)/shard_map/pallas_call | solution.py:82
  40.9 27.0 %all_to_all.10 = f32[16,128,128]{2,1,0:T(8,128)S(1)} all-to-all(f32[16,128,128]{2,1,0:T(8,128)} %shard_map.55), channel_id=1, replica_groups=mesh['row'=16,'col'=16] {'col'}, dimensions={0} | all-to-all | bytes 2097152 | tf_op jit(solution)/shard_map/all_to_all | solution.py:109
  68.0 0.7 reduce_sum.9
Async XLA Ops:
  1.4 33.3 %all-to-all-start = ((bf16[16,32,128]{2,1,0:T(8,128)(2,1)}), bf16[16,32,128]{2,1,0:T(8,128)(2,1)S(1)}, u32[]{:S(2)}, u32[]{:S(2)}) async-start(bf16[16,32,128]{2,1,0:T(8,128)(2,1)} %broadcast_in_dim.2), calls=%async_computation | async-start | bytes 262144 | tf_op jit(solution)/shard_map/all_to_all | solution.py:17
  34.7 0.6 copy-start

commit v5 on v4

--- a/solution.py
+++ b/solution.py
@@ -18,14 +18,14 @@
     return gathered.reshape(-1, piece.shape[-1])
 
 
-def slot_kernel(coords_ref, count_ref, blocks_hbm, doc_ref, ctx_ref, out_ref, held, sems):
+def slot_kernel(coords_ref, blocks_hbm, doc_ref, ctx_ref, out_ref, held, sems):
     n_doc = doc_ref.shape[0]
     n_ctx = ctx_ref.shape[0]
     n_q = out_ref.shape[0]
     slots = blocks_hbm.shape[0]
     pieces = held.shape[1]
     piece = held.shape[-1]
-    used = jnp.clip(count_ref[0], 0, slots)
+    used = jnp.clip(coords_ref[3, 0], 0, slots)
 
     def fetch(slot, part):
         return pltpu.make_async_copy(
@@ -70,7 +70,7 @@
     lax.fori_loop(0, used, step, 0)
 
 
-def slot_terms(own_blocks, own_coords, used, doc_blocks, ctx_blocks, n_q):
+def slot_terms(own_blocks, table, doc_blocks, ctx_blocks, n_q):
     slots, rows, width = own_blocks.shape
     rank = doc_blocks.shape[-1]
     pieces = 4
@@ -83,7 +83,6 @@
         slot_kernel,
         in_specs=[
             pl.BlockSpec(memory_space=pltpu.SMEM),
-            pl.BlockSpec(memory_space=pltpu.SMEM),
             pl.BlockSpec(memory_space=pl.ANY),
             pl.BlockSpec(memory_space=pltpu.VMEM),
             pl.BlockSpec(memory_space=pltpu.VMEM),
@@ -95,17 +94,25 @@
             pltpu.SemaphoreType.DMA((2, pieces)),
         ],
         cost_estimate=cost,
-    )(own_coords.T, used.reshape(-1), own_blocks, doc_blocks, ctx_blocks)
+    )(table, own_blocks, doc_blocks, ctx_blocks)
+
+
+def slot_table(coords, counts):
+    ids = coords[0, 0].T
+    used = jnp.broadcast_to(counts[0].reshape(1, 1), (1, ids.shape[1]))
+    return jnp.concatenate([ids, used], axis=0)
 
 
 def body(blocks, coords, counts, doc_factor, ctx_factor):
+    table = slot_table(coords, counts)
+    table, ctx_factor = lax.optimization_barrier((table, ctx_factor))
     doc_slab = lax.all_gather(doc_factor, "row", axis=0, tiled=True)
     ctx_all = gather_rows(ctx_factor, "col")
     rank = doc_slab.shape[1]
     n_q = QBC * lax.axis_size("col")
     doc_blocks = doc_slab.reshape(-1, BD, rank)
     ctx_blocks = ctx_all.reshape(-1, BK, rank)
-    parts = slot_terms(blocks[0, 0], coords[0, 0], counts[0], doc_blocks, ctx_blocks, n_q)
+    parts = slot_terms(blocks[0, 0], table, doc_blocks, ctx_blocks, n_q)
     return lax.all_to_all(parts, "col", 0, 0, tiled=True).sum(axis=0)
 
 

time: 69.1 us -> 68 us (0.984); the launches traced: 68.7 us -> 66.7 us
  Pallas kernels: 5.58 us -> 4.37 us
  blocking collectives: 50.9 us -> 50.1 us
    pallas_call x1, Pallas kernels: 5.58 us -> 4.37 us  [slot_terms(): pl.pallas_call(slot_kernel, in_specs=[pl.BlockSpec(memory_space=pltpu.SME...]
    all_to_all x1, blocking collectives: 27 us -> 26.3 us  [body(): return lax.all_to_all(parts, 'col', 0, 0, tiled=True).sum(axis=0)]
  transfers between devices with their start and end apart: 1 -> 1, of which waited for: 0 -> 0; matrix products, arithmetic and copies ran while one was open for 2% -> 0% of each run, Pallas kernels for 0% -> 0%
where the time goes in v5:
time: 68 us; the launch traced here: 66.7 us
  blocking collectives  50.1 us (74%)
  starting transfers between devices  7.57 us (11%)
  Pallas kernels  4.37 us (6%)
  local copies, waits for them, and re-layouts  3.28 us (5%)
  other arithmetic  0.69 us (1%)
    all_to_all x1, blocking collectives, body(): return lax.all_to_all(parts, 'col', 0, 0, tiled=True).sum(axis=0)  26.3 us
    all_gather x1, blocking collectives, body(): doc_slab = lax.all_gather(doc_factor, 'row', axis=0, tiled=True)  23.8 us
    all_to_all x1, starting transfers between devices, gather_rows(): gathered = lax.all_to_all(copies, axis, 0, 0, tiled=True)  7.57 us
    pallas_call x1, Pallas kernels, slot_terms(): pl.pallas_call(slot_kernel, in_specs=[pl.BlockSpec(memory_space=pltpu.SME...  4.37 us
    broadcast_in_dim x1, local copies, waits for them, and re-layouts, gather_rows(): copies = jnp.broadcast_to(piece[None], (lax.axis_size(axis),) + piece.shape)  1.36 us
  transfers between devices with their start and end apart: 1, of which 0 were waited for; matrix products, arithmetic and copies ran while one was open for 0% of the time, Pallas kernels for 0%

profile of v5, /device:TPU:1, one launch (start us, length us, event | category | flops | bytes accessed | tf_op | source)
XLA Modules:
  0.0 66.7 jit_solution(3796799879198033327)
XLA Ops:
  0.7 0.7 %copy.8 = s32[1,1,5,3]{2,3,1,0:T(4,128)S(1)} copy(s32[1,1,5,3]{2,1,3,0:T(1,128)} %param.6) | data formatting | bytes 120
  1.3 0.6 concatenate.3.coords_ref
  1.9 1.4 %broadcast_in_dim.5 = bf16[16,32,128]{2,1,0:T(8,128)(2,1)} broadcast(bf16[32,128]{1,0:T(8,128)(2,1)} %param.9), dimensions={1,2} | broadcast | bytes 139264 | tf_op jit(solution)/shard_map/broadcast_in_dim | solution.py:16
  3.3 7.6 %all-to-all-start = ((bf16[16,32,128]{2,1,0:T(8,128)(2,1)}), bf16[16,32,128]{2,1,0:T(8,128)(2,1)S(1)}, u32[]{:S(2)}, u32[]{:S(2)}) async-start(bf16[16,32,128]{2,1,0:T(8,128)(2,1)} %broadcast_in_dim.5), calls=%async_computation | async-start | bytes 262144 | tf_op jit(solution)/shard_map/all_to_all | solution.py:17
  10.9 23.8 %all_gather.3 = bf16[2048,128]{1,0:T(8,128)(2,1)} all-gather(bf16[128,128]{1,0:T(8,128)(2,1)} %param.8), channel_id=1, replica_groups=mesh['row'=16,'col'=16] {'row'}, dimensions={0}, use_global_device_ids=true | all-gather | bytes 557056 | tf_op jit(solution)/shard_map/all_gather | solution.py:109
  34.7 0.0 all-to-all-done
  34.7 0.0 copy-start
  34.7 0.6 copy-done
  35.4 4.4 %shard_map.55 = f32[16,128,128]{2,1,0:T(8,128)} custom-call(s32[4,5]{1,0:T(4,128)} %concatenate.3.coords_ref, bf16[5,128,8192]{2,1,0:T(8,128)(2,1)} %bitcast.10, bf16[16,128,128]{2,1,0:T(8,128)(2,1)} %bitcast.11, bf16[8,64,128]{2,1,0:T(8,128)(2,1)} %bitcast.12), custom_call_target="tpu_custom_call" | custom-call | flops 1342177280 | bytes 11534336 | tf_op jit(solution)/shard_map/pallas_call | solution.py:82
  39.7 26.3 %all_to_all.10 = f32[16,128,128]{2,1,0:T(8,128)S(1)} all-to-all(f32[16,128,128]{2,1,0:T(8,128)} %shard_map.55), channel_id=1, replica_groups=mesh['row'=16,'col'=16] {'col'}, dimensions={0} | all-to-all | bytes 2097152 | tf_op jit(solution)/shard_map/all_to_all | solution.py:116
  66.0 0.7 %reduce_sum.9 = f32[128,128]{1,0:T(8,128)} reduce(f32[16,128,128]{2,1,0:T(8,128)S(1)} %all_to_all.10, f32[]{:T(128)} %constant.0.clone.1), dimensions={0}, to_apply=%region_0.0 | reduce | flops 245760 | bytes 1114116 | tf_op jit(solution)/shard_map/reduce_sum | solution.py:116
Async XLA Ops:
  3.3 31.4 %all-to-all-start = ((bf16[16,32,128]{2,1,0:T(8,128)(2,1)}), bf16[16,32,128]{2,1,0:T(8,128)(2,1)S(1)}, u32[]{:S(2)}, u32[]{:S(2)}) async-start(bf16[16,32,128]{2,1,0:T(8,128)(2,1)} %broadcast_in_dim.5), calls=%async_computation | async-start | bytes 262144 | tf_op jit(solution)/shard_map/all_to_all | solution.py:17
  34.7 0.7 copy-start

commit v6 on v4

--- a/solution.py
+++ b/solution.py
@@ -10,6 +10,7 @@
 BK = 64
 QBC = 1
 DOC_CHUNK = 16
+VMEM_LIMIT = 50 * 1024 * 1024
 
 
 def gather_rows(piece, axis):
@@ -94,6 +95,7 @@
             pltpu.VMEM((2, pieces, rows, width // pieces), own_blocks.dtype),
             pltpu.SemaphoreType.DMA((2, pieces)),
         ],
+        compiler_params=pltpu.CompilerParams(vmem_limit_bytes=VMEM_LIMIT),
         cost_estimate=cost,
     )(own_coords.T, used.reshape(-1), own_blocks, doc_blocks, ctx_blocks)
 

time: 69.1 us -> 62.1 us (0.90)
  Pallas kernels: 5.58 us -> 2.95 us
  blocking collectives: 50.9 us -> 48.3 us
  local copies, waits for them, and re-layouts: 3.27 us -> 2.03 us
    pallas_call x1, Pallas kernels: 5.58 us -> 2.95 us  [slot_terms(): pl.pallas_call(slot_kernel, in_specs=[pl.BlockSpec(memory_space=pltpu.SME...]
    all_gather x1, blocking collectives: 23.8 us -> 22.4 us  [body(): doc_slab = lax.all_gather(doc_factor, 'row', axis=0, tiled=True)]
    unnamed x3 -> x1, local copies, waits for them, and re-layouts: 1.91 us -> 0.68 us
    all_to_all x1, blocking collectives: 27 us -> 25.8 us  [body(): return lax.all_to_all(parts, 'col', 0, 0, tiled=True).sum(axis=0)]
  transfers between devices with their start and end apart: 1 -> 1, of which waited for: 0 -> 0; matrix products, arithmetic and copies ran while one was open for 2% -> 1% of each run, Pallas kernels for 0% -> 0%
where the time goes in v6:
time: 62.1 us; the launch traced here: 62.2 us
  blocking collectives  48.3 us (78%)
  starting transfers between devices  7.57 us (12%)
  Pallas kernels  2.95 us (5%)
  local copies, waits for them, and re-layouts  2.03 us (3%)
  other arithmetic  0.69 us (1%)
  between operations  0.67 us (1%)
    all_to_all x1, blocking collectives, body(): return lax.all_to_all(parts, 'col', 0, 0, tiled=True).sum(axis=0)  25.8 us
    all_gather x1, blocking collectives, body(): doc_slab = lax.all_gather(doc_factor, 'row', axis=0, tiled=True)  22.4 us
    all_to_all x1, starting transfers between devices, gather_rows(): gathered = lax.all_to_all(copies, axis, 0, 0, tiled=True)  7.57 us
    pallas_call x1, Pallas kernels, slot_terms(): pl.pallas_call(slot_kernel, in_specs=[pl.BlockSpec(memory_space=pltpu.SME...  2.95 us
    broadcast_in_dim x1, local copies, waits for them, and re-layouts, gather_rows(): copies = jnp.broadcast_to(piece[None], (lax.axis_size(axis),) + piece.shape)  1.35 us
  transfers between devices with their start and end apart: 1, of which 0 were waited for; matrix products, arithmetic and copies ran while one was open for 1% of the time, Pallas kernels for 0%

profile of v6, /device:TPU:1, one launch (start us, length us, event | category | flops | bytes accessed | tf_op | source)
XLA Modules:
  0.0 62.2 jit_solution(12630681381201989873)
XLA Ops:
  0.0 1.4 %broadcast_in_dim.2 = bf16[16,32,128]{2,1,0:T(8,128)(2,1)} broadcast(bf16[32,128]{1,0:T(8,128)(2,1)} %param.9), dimensions={1,2} | broadcast | bytes 139264 | tf_op jit(solution)/shard_map/broadcast_in_dim | solution.py:17
  1.4 7.6 %all-to-all-start = ((bf16[16,32,128]{2,1,0:T(8,128)(2,1)}), bf16[16,32,128]{2,1,0:T(8,128)(2,1)S(1)}, u32[]{:S(2)}, u32[]{:S(2)}) async-start(bf16[16,32,128]{2,1,0:T(8,128)(2,1)} %broadcast_in_dim.2), calls=%async_computation | async-start | bytes 262144 | tf_op jit(solution)/shard_map/all_to_all | solution.py:18
  8.9 22.4 %all_gather.3 = bf16[2048,128]{1,0:T(8,128)(2,1)S(1)} all-gather(bf16[128,128]{1,0:T(8,128)(2,1)} %param.8), channel_id=1, replica_groups=mesh['row'=16,'col'=16] {'row'}, dimensions={0}, use_global_device_ids=true | all-gather | bytes 557056 | tf_op jit(solution)/shard_map/all_gather | solution.py:104
  32.0 0.7 %copy.8 = s32[1,1,5,3]{2,3,1,0:T(4,128)S(1)} copy(s32[1,1,5,3]{2,1,3,0:T(1,128)} %param.6) | data formatting | bytes 120
  32.7 0.0 all-to-all-done
  32.7 2.9 %shard_map.55 = f32[16,128,128]{2,1,0:T(8,128)S(1)} custom-call(s32[3,5]{1,0:T(4,128)S(1)} %bitcast.12, s32[1]{0:T(128)} %bitcast.9.count_ref, bf16[5,128,8192]{2,1,0:T(8,128)(2,1)} %bitcast.13, bf16[16,128,128]{2,1,0:T(8,128)(2,1)S(1)} %bitcast.10, bf16[8,64,128]{2,1,0:T(8,128)(2,1)S(1)} %bitcast.11), custom_call_target="tpu_custom_call" | custom-call | flops 1342177280 | bytes 11534336 | tf_op jit(solution)/shard_map/pallas_call | solution.py:83
  35.7 25.8 %all_to_all.10 = f32[16,128,128]{2,1,0:T(8,128)S(1)} all-to-all(f32[16,128,128]{2,1,0:T(8,128)S(1)} %shard_map.55), channel_id=1, replica_groups=mesh['row'=16,'col'=16] {'col'}, dimensions={0} | all-to-all | bytes 2097152 | tf_op jit(solution)/shard_map/all_to_all | solution.py:111
  61.5 0.7 %reduce_sum.9 = f32[128,128]{1,0:T(8,128)} reduce(f32[16,128,128]{2,1,0:T(8,128)S(1)} %all_to_all.10, f32[]{:T(128)} %constant.0.clone.1), dimensions={0}, to_apply=%region_0.0 | reduce | flops 245760 | bytes 1114116 | tf_op jit(solution)/shard_map/reduce_sum | solution.py:111
Async XLA Ops:
  1.4 31.4 %all-to-all-start = ((bf16[16,32,128]{2,1,0:T(8,128)(2,1)}), bf16[16,32,128]{2,1,0:T(8,128)(2,1)S(1)}, u32[]{:S(2)}, u32[]{:S(2)}) async-start(bf16[16,32,128]{2,1,0:T(8,128)(2,1)} %broadcast_in_dim.2), calls=%async_computation | async-start | bytes 262144 | tf_op jit(solution)/shard_map/all_to_all | solution.py:18

commit v7 on v5

--- a/solution.py
+++ b/solution.py
@@ -10,6 +10,7 @@
 BK = 64
 QBC = 1
 DOC_CHUNK = 16
+VMEM_LIMIT = 50 * 1024 * 1024
 
 
 def gather_rows(piece, axis):
@@ -73,7 +74,7 @@
 def slot_terms(own_blocks, table, doc_blocks, ctx_blocks, n_q):
     slots, rows, width = own_blocks.shape
     rank = doc_blocks.shape[-1]
-    pieces = 4
+    pieces = 2
     cost = pl.CostEstimate(
         flops=2 * slots * rows * width * rank,
         bytes_accessed=own_blocks.size * 2 + n_q * rows * rank * 4,
@@ -93,6 +94,7 @@
             pltpu.VMEM((2, pieces, rows, width // pieces), own_blocks.dtype),
             pltpu.SemaphoreType.DMA((2, pieces)),
         ],
+        compiler_params=pltpu.CompilerParams(vmem_limit_bytes=VMEM_LIMIT),
         cost_estimate=cost,
     )(table, own_blocks, doc_blocks, ctx_blocks)
 

time: 68 us -> 63.3 us (0.931); the launches traced: 66.7 us -> 62.8 us
  blocking collectives: 50.1 us -> 48.1 us
  local copies, waits for them, and re-layouts: 3.28 us -> 2.04 us
  Pallas kernels: 4.37 us -> 3.65 us
    all_gather x1, blocking collectives: 23.8 us -> 22.4 us  [body(): doc_slab = lax.all_gather(doc_factor, 'row', axis=0, tiled=True)]
    pallas_call x1, Pallas kernels: 4.37 us -> 3.65 us  [slot_terms(): pl.pallas_call(slot_kernel, in_specs=[pl.BlockSpec(memory_space=pltpu.SME...]
where the time goes in v7:
time: 63.3 us; the launch traced here: 62.8 us
  blocking collectives  48.1 us (76%)
  starting transfers between devices  7.57 us (12%)
  Pallas kernels  3.65 us (6%)
  local copies, waits for them, and re-layouts  2.04 us (3%)
  other arithmetic  0.69 us (1%)
  between operations  0.67 us (1%)
    all_to_all x1, blocking collectives, body(): return lax.all_to_all(parts, 'col', 0, 0, tiled=True).sum(axis=0)  25.7 us
    all_gather x1, blocking collectives, body(): doc_slab = lax.all_gather(doc_factor, 'row', axis=0, tiled=True)  22.4 us
    all_to_all x1, starting transfers between devices, gather_rows(): gathered = lax.all_to_all(copies, axis, 0, 0, tiled=True)  7.57 us
    pallas_call x1, Pallas kernels, slot_terms(): pl.pallas_call(slot_kernel, in_specs=[pl.BlockSpec(memory_space=pltpu.SME...  3.65 us
    broadcast_in_dim x1, local copies, waits for them, and re-layouts, gather_rows(): copies = jnp.broadcast_to(piece[None], (lax.axis_size(axis),) + piece.shape)  1.35 us
  transfers between devices with their start and end apart: 1, of which 0 were waited for; matrix products, arithmetic and copies ran while one was open for 0% of the time, Pallas kernels for 0%

profile of v7, /device:TPU:1, one launch (start us, length us, event | category | flops | bytes accessed | tf_op | source)
XLA Modules:
  0.0 62.8 jit_solution(12154566133696157866)
XLA Ops:
  0.7 0.7 %copy.8 = s32[1,1,5,3]{2,3,1,0:T(4,128)S(1)} copy(s32[1,1,5,3]{2,1,3,0:T(1,128)} %param.6) | data formatting | bytes 120
  1.3 1.4 %broadcast_in_dim.5 = bf16[16,32,128]{2,1,0:T(8,128)(2,1)} broadcast(bf16[32,128]{1,0:T(8,128)(2,1)} %param.9), dimensions={1,2} | broadcast | bytes 139264 | tf_op jit(solution)/shard_map/broadcast_in_dim | solution.py:17
  2.7 7.6 %all-to-all-start = ((bf16[16,32,128]{2,1,0:T(8,128)(2,1)}), bf16[16,32,128]{2,1,0:T(8,128)(2,1)S(1)}, u32[]{:S(2)}, u32[]{:S(2)}) async-start(bf16[16,32,128]{2,1,0:T(8,128)(2,1)} %broadcast_in_dim.5), calls=%async_computation | async-start | bytes 262144 | tf_op jit(solution)/shard_map/all_to_all | solution.py:18
  10.3 22.4 %all_gather.3 = bf16[2048,128]{1,0:T(8,128)(2,1)S(1)} all-gather(bf16[128,128]{1,0:T(8,128)(2,1)} %param.8), channel_id=1, replica_groups=mesh['row'=16,'col'=16] {'row'}, dimensions={0}, use_global_device_ids=true | all-gather | bytes 557056 | tf_op jit(solution)/shard_map/all_gather | solution.py:111
  32.7 0.0 all-to-all-done
  32.7 3.7 %shard_map.55 = f32[16,128,128]{2,1,0:T(8,128)S(1)} custom-call(s32[4,5]{1,0:T(4,128)S(1)} %concatenate.3.coords_ref, bf16[5,128,8192]{2,1,0:T(8,128)(2,1)} %bitcast.12, bf16[16,128,128]{2,1,0:T(8,128)(2,1)S(1)} %bitcast.10, bf16[8,64,128]{2,1,0:T(8,128)(2,1)S(1)} %bitcast.11), custom_call_target="tpu_custom_call" | custom-call | flops 1342177280 | bytes 11534336 | tf_op jit(solution)/shard_map/pallas_call | solution.py:83
  36.4 25.7 %all_to_all.10 = f32[16,128,128]{2,1,0:T(8,128)S(1)} all-to-all(f32[16,128,128]{2,1,0:T(8,128)S(1)} %shard_map.55), channel_id=1, replica_groups=mesh['row'=16,'col'=16] {'col'}, dimensions={0} | all-to-all | bytes 2097152 | tf_op jit(solution)/shard_map/all_to_all | solution.py:118
  62.1 0.7 %reduce_sum.9 = f32[128,128]{1,0:T(8,128)} reduce(f32[16,128,128]{2,1,0:T(8,128)S(1)} %all_to_all.10, f32[]{:T(128)} %constant.0.clone.1), dimensions={0}, to_apply=%region_0.0 | reduce | flops 245760 | bytes 1114116 | tf_op jit(solution)/shard_map/reduce_sum | solution.py:118
  (1 shorter events, 0.0 us)
Async XLA Ops:
  2.7 30.0 %all-to-all-start = ((bf16[16,32,128]{2,1,0:T(8,128)(2,1)}), bf16[16,32,128]{2,1,0:T(8,128)(2,1)S(1)}, u32[]{:S(2)}, u32[]{:S(2)}) async-start(bf16[16,32,128]{2,1,0:T(8,128)(2,1)} %broadcast_in_dim.5), calls=%async_computation | async-start | bytes 262144 | tf_op jit(solution)/shard_map/all_to_all | solution.py:18
